TPU v7x, 16 devices: a whole 2x2x2 slice. The times are simulated.
16 devices in a mesh: data: 16 (over z, y, x, core).
Axes of the slice: x: 2, y: 2, z: 2, core: 2. Of those that a mesh axis runs over, the one named last changes fastest.
Arguments:
- h_a: bfloat16 [16384, 384], P('data')
- h_b: bfloat16 [16384, 384], P('data')
- w_one: bfloat16 [384, 2048], replicated
- w_two: bfloat16 [2048, 2048], replicated
- w_three: bfloat16 [2048, 2048], replicated
- gain_one: float32 [2048], replicated
- bias_one: float32 [2048], replicated
- gain_two: float32 [2048], replicated
- bias_two: float32 [2048], replicated
Outputs:
- output 1: float32 [], replicated
- output 2: float32 [384, 2048], replicated
- output 3: float32 [2048, 2048], replicated
- output 4: float32 [2048, 2048], replicated
- output 5: float32 [2048], replicated
- output 6: float32 [2048], replicated
- output 7: float32 [2048], replicated
- output 8: float32 [2048], replicated
All inputs are finite; a program needn't handle non-finite values.
Results may differ from a plain program's by a relative error of at most 0.001.
Values are sent between devices in bfloat16 or wider.
A program may use at most 1 GiB of HBM per device.

v0:
```python
import jax
import jax.numpy as jnp
from jax import lax
from jax.sharding import PartitionSpec as P

BN_EPS = 1e-5
STD_EPS = 1e-4
INV_WEIGHT = 2.0
VAR_WEIGHT = 1.0
COV_WEIGHT = 2.0


def layer_forward(x_in, weight, gain_vec, bias_vec, all_rows):
    pre_act = jnp.einsum('vnk,kd->vnd', x_in, weight, preferred_element_type=jnp.float32)
    moments = lax.psum(jnp.stack([jnp.sum(pre_act, axis=1), jnp.sum(pre_act * pre_act, axis=1)]), 'data')
    col_mean = moments[0] / all_rows
    col_var = moments[1] / all_rows - col_mean * col_mean
    inv_std = lax.rsqrt(col_var + BN_EPS)[:, None, :]
    normed = (pre_act - col_mean[:, None, :]) * inv_std
    act_val = gain_vec * normed + bias_vec
    return jnp.maximum(act_val, 0.0).astype(jnp.bfloat16), normed, act_val, inv_std


def layer_backward(d_out, normed, act_val, inv_std, gain_vec, all_rows):
    d_act = jnp.where(act_val > 0.0, d_out, 0.0)
    stat_sums = lax.psum(jnp.stack([jnp.sum(d_act, axis=1), jnp.sum(d_act * normed, axis=1)]), 'data')
    d_pre = inv_std * gain_vec * (d_act - stat_sums[0][:, None, :] / all_rows - normed * (stat_sums[1][:, None, :] / all_rows))
    return d_pre.astype(jnp.bfloat16), jnp.sum(stat_sums[1], axis=0), jnp.sum(stat_sums[0], axis=0)


def loss_from_stats(z_views, z_diff, col_sum, gram_mat, sq_sum, all_rows):
    col_mu = col_sum / all_rows
    cov_mat = (gram_mat - all_rows * col_mu[:, :, None] * col_mu[:, None, :]) / (all_rows - 1)
    diag_var = jnp.diagonal(cov_mat, axis1=1, axis2=2)
    std_vec = jnp.sqrt(diag_var + STD_EPS)
    hinge_on = (std_vec < 1.0).astype(jnp.float32)
    loss_val = (INV_WEIGHT * sq_sum / all_rows
                + VAR_WEIGHT * jnp.sum(jnp.maximum(1.0 - std_vec, 0.0))
                + COV_WEIGHT * (jnp.sum(cov_mat * cov_mat) - jnp.sum(diag_var * diag_var)))
    proj_dim = cov_mat.shape[-1]
    eye_mask = lax.broadcasted_iota(jnp.int32, (proj_dim, proj_dim), 0) == lax.broadcasted_iota(jnp.int32, (proj_dim, proj_dim), 1)
    grad_cov = jnp.where(eye_mask, (-VAR_WEIGHT * hinge_on / (2.0 * std_vec))[:, None, :], (2.0 * COV_WEIGHT) * cov_mat)
    g_hat = grad_cov.astype(jnp.bfloat16)
    row_part = jnp.einsum('woe,wef->wof', z_views, g_hat, preferred_element_type=jnp.float32)
    mean_part = jnp.einsum('vd,vde->ve', col_mu, g_hat.astype(jnp.float32), precision=lax.Precision.HIGHEST)
    d_inv = (2.0 * INV_WEIGHT / all_rows) * z_diff
    d_z = ((2.0 / (all_rows - 1)) * (row_part - mean_part[:, None, :]) + jnp.stack([d_inv, -d_inv])).astype(jnp.bfloat16)
    return loss_val, d_z


def solution(mesh):
    group_devs = mesh.shape['data']

    def local_step(h_a, h_b, w_one, w_two, w_three, gain_one, bias_one, gain_two, bias_two):
        all_rows = h_a.shape[0] * group_devs
        view_feats = jnp.stack([h_a, h_b])
        hidden_one, normed_one, act_one, inv_one = layer_forward(view_feats, w_one, gain_one, bias_one, all_rows)
        hidden_two, normed_two, act_two, inv_two = layer_forward(hidden_one, w_two, gain_two, bias_two, all_rows)
        z_views = jnp.einsum('vnk,kd->vnd', hidden_two, w_three, preferred_element_type=jnp.float32).astype(jnp.bfloat16)
        z_diff = z_views[0].astype(jnp.float32) - z_views[1].astype(jnp.float32)
        col_sum, gram_mat, sq_sum = lax.psum(
            (jnp.sum(z_views, axis=1, dtype=jnp.float32),
             jnp.einsum('woe,wof->wef', z_views, z_views, preferred_element_type=jnp.float32),
             jnp.sum(z_diff * z_diff)), 'data')
        loss_val, d_z = loss_from_stats(z_views, z_diff, col_sum, gram_mat, sq_sum, all_rows)
        grad_three = jnp.einsum('vnk,vnd->kd', hidden_two, d_z, preferred_element_type=jnp.float32)
        d_hidden_two = jnp.einsum('vnd,kd->vnk', d_z, w_three, preferred_element_type=jnp.float32)
        d_pre_two, gain_grad_two, bias_grad_two = layer_backward(d_hidden_two, normed_two, act_two, inv_two, gain_two, all_rows)
        grad_two = jnp.einsum('vnk,vnd->kd', hidden_one, d_pre_two, preferred_element_type=jnp.float32)
        d_hidden_one = jnp.einsum('vnd,kd->vnk', d_pre_two, w_two, preferred_element_type=jnp.float32)
        d_pre_one, gain_grad_one, bias_grad_one = layer_backward(d_hidden_one, normed_one, act_one, inv_one, gain_one, all_rows)
        grad_one = jnp.einsum('vnf,vnd->fd', view_feats, d_pre_one, preferred_element_type=jnp.float32)
        grad_one, grad_two, grad_three = lax.psum((grad_one, grad_two, grad_three), 'data')
        return loss_val, grad_one, grad_two, grad_three, gain_grad_one, bias_grad_one, gain_grad_two, bias_grad_two

    row_spec = P('data', None)
    return jax.shard_map(local_step, mesh=mesh,
                         in_specs=(row_spec, row_spec, P(), P(), P(), P(), P(), P(), P()),
                         out_specs=(P(), P(), P(), P(), P(), P(), P(), P()),
                         check_vma=False)
```

profile of v0, /device:TPU:0, one launch (start us, length us, event | category | flops | bytes accessed | tf_op | source)
XLA Modules:
  0.0 1211.0 jit_solution(5618457695561391916)
XLA Ops:
  8.6 10.0 fusion.45
  18.7 34.8 %psum.70 = f32[2,2,2048]{2,1,0:T(2,128)S(1)} all-reduce(f32[2,2,2048]{2,1,0:T(2,128)S(1)} %pad_maximum_fusion.3), channel_id=1, replica_groups=mesh['data'=16] {'data'}, use_global_device_ids=true, to_apply=%region_2.0 | all-reduce | flops 8192 | bytes 65536 | tf_op jit(solution)/shard_map/psum | solution.py:15
  54.2 24.9 %fusion.44 = (f32[2,2048]{1,0:T(2,128)S(1)}, f32[2,2048]{1,0:T(2,128)S(1)}, f32[2,1024,2048]{2,1,0:T(8,128)}) fusion(bf16[2048,2048]{1,0:T(8,128)(2,1)} %param.12, f32[2,1024,2048]{2,1,0:T(8,128)} %get-tuple-element.42, f32[2048]{0:T(1024)S(1)} %copy-done.24, f32[2,2048]{1,0:T(2,128)S(1)} %get-tuple-element.37, f32[2,2048]{1,0:T(2,128)S(1)} %fusion.34, ...), kind=kOutput, calls=%fused_computation.87 | convolution fusion | flops 17217609728 | bytes 42024960 | tf_op jit(solution)/shard_map/vnk,kd->vnd/dot_general | solution.py:14
  79.1 33.0 %psum.71 = f32[2,2,2048]{2,1,0:T(2,128)S(1)} all-reduce(f32[2,2,2048]{2,1,0:T(2,128)S(1)} %pad_maximum_fusion.4), channel_id=1, replica_groups=mesh['data'=16] {'data'}, use_global_device_ids=true, to_apply=%region_5.0 | all-reduce | flops 8192 | bytes 65536 | tf_op jit(solution)/shard_map/psum | solution.py:15
  112.8 22.8 %convert_reduce_fusion = (f32[2,2048]{1,0:T(2,128)S(1)}, bf16[2,1024,2048]{2,1,0:T(8,128)(2,1)S(1)}) fusion(bf16[2048,2048]{1,0:T(8,128)(2,1)} %param.13, f32[2,1024,2048]{2,1,0:T(8,128)} %get-tuple-element.43, f32[2048]{0:T(1024)S(1)} %copy-done.22, f32[2,2048]{1,0:T(2,128)S(1)} %get-tuple-element.39, f32[2,2048]{1,0:T(2,128)S(1)} %fusion.28, ...), kind=kOutput, calls=%fused_computation.12 | convolution fusion | flops 17217613824 | bytes 33619968 | tf_op jit(solution)/shard_map/vnk,kd->vnd/dot_general | solution.py:59
  138.9 22.1 %fusion.47 = f32[2,2048,2048]{2,1,0:T(8,128)} fusion(bf16[2,1024,2048]{2,1,0:T(8,128)(2,1)S(1)} %get-tuple-element.45), kind=kOutput, calls=%fused_computation.89 | convolution fusion | flops 17179869184 | bytes 41943040 | tf_op jit(solution)/shard_map/woe,wof->wef/dot_general | solution.py:63
  161.1 34.0 %psum.74 = f32[2,2048]{1,0:T(2,128)S(1)} all-reduce(f32[2,2048]{1,0:T(2,128)S(1)} %get-tuple-element.44), channel_id=1, replica_groups=mesh['data'=16] {'data'}, use_global_device_ids=true, to_apply=%region_10.0 | all-reduce | flops 4096 | bytes 32768 | tf_op jit(solution)/shard_map/psum | solution.py:61
  199.3 10.1 fusion.15
  209.3 270.9 %all-reduce.5.cloned.1.call-done = f32[2,2048,2048]{2,1,0:T(8,128)} async-done(((f32[2,2048,2048]{2,1,0:T(8,128)}), f32[2,2048,2048]{2,1,0:T(8,128)}) %all-reduce.5.cloned.1.call-update) | async-done | bytes 33554448 | tf_op jit(solution)/shard_map/psum | solution.py:61
  480.2 23.6 %multiply_reduce_fusion = (f32[]{:T(128)}, f32[2,2048,2048]{2,1,0:T(8,128)}) fusion(f32[2,2048,2048]{2,1,0:T(8,128)} %all-reduce.5.cloned.1.call-done, f32[2,2048]{1,0:T(2,128)S(1)} %get-tuple-element.40, f32[2,2048]{1,0:T(2,128)S(1)} %psum.74), kind=kLoop, calls=%fused_computation.2 | loop fusion | flops 41943040 | bytes 67141632 | tf_op jit(solution)/shard_map/reduce_sum | solution.py:39
  503.8 55.0 %copy.23 = f32[2,2048,2048]{2,0,1:T(2,128)} copy(f32[2,2048,2048]{2,1,0:T(8,128)} %get-tuple-element.28) | data formatting | bytes 67108864 | tf_op jit(solution)/shard_map/div | solution.py:33
  558.8 24.1 %gather_fusion = f32[2048,2]{0,1:T(2,128)S(1)} fusion(f32[2,2048,2048]{2,0,1:T(2,128)} %copy.23, s32[2048]{0:T(1024)S(1)} %bitcast.100), kind=kCustom, calls=%fused_computation | custom fusion | bytes 49152 | tf_op jit(solution)/shard_map/jit(diagonal)/gather | solution.py:34
  582.9 16.9 %fusion.35 = f32[2,1,2048]{2,1,0:T(1,128)S(1)} fusion(f32[2,2048,1]{1,0,2:T(2,128)S(1)} %get-tuple-element.41, f32[2,2048,2048]{2,1,0:T(8,128)} %all-reduce.5.cloned.1.call-done, bf16[2,2048]{1,0:T(2,128)(2,1)S(1)} %fusion.37, f32[2,2048]{1,0:T(2,128)S(1)} %get-tuple-element.40, f32[2,2048]{1,0:T(2,128)S(1)} %psum.74, pred[2048,2048]{1,0:T(8,128)(4,1)} %iota_compare_fusion), kind=kOutput, calls=%fused_computation.65 | convolution fusion | flops 134217728 | bytes 37822464 | tf_op jit(solution)/shard_map/vd,vde->ve/dot_general | solution.py:45
  599.9 29.1 %fusion.1 = bf16[2,1024,2048]{2,1,0:T(8,128)(2,1)} fusion(f32[1,1024,2048]{2,1,0:T(8,128)} %get-tuple-element.30, f32[1,1024,2048]{2,1,0:T(8,128)} %get-tuple-element.29, f32[2,2048]{1,0:T(2,128)S(1)} %bitcast.107, bf16[2,1024,2048]{2,1,0:T(8,128)(2,1)} %copy-done.3, f32[2,2048,2048]{2,1,0:T(8,128)} %all-reduce.5.cloned.1.call-done, ...), kind=kOutput, calls=%fused_computation.6 | convolution fusion | flops 17234395136 | bytes 71360512 | tf_op jit(solution)/shard_map/woe,wef->wof/dot_general | solution.py:44
  629.0 25.3 %convolution_bitcast_fusion = f32[2048,2048]{1,0:T(8,128)} fusion(bf16[2,1024,2048]{2,1,0:T(8,128)(2,1)} %fusion.1, f32[2,1024,2048]{2,1,0:T(8,128)} %get-tuple-element.43, f32[2048]{0:T(1024)S(1)} %copy-done.23, f32[2,2048]{1,0:T(2,128)S(1)} %copy-done.17, f32[2,2048]{1,0:T(2,128)S(1)} %copy-done.14, f32[2048]{0:T(1024)S(1)} %copy-done.19), kind=kOutput, calls=%fused_computation.23 | convolution fusion | flops 17205035008 | bytes 41992192 | tf_op jit(solution)/shard_map/vnk,vnd->kd/dot_general | solution.py:66
  654.3 28.7 %fusion.43 = (f32[2,2048]{1,0:T(2,128)S(1)}, f32[2,2048]{1,0:T(2,128)S(1)}, f32[2,1024,2048]{2,1,0:T(8,128)}) fusion(f32[2,2048]{1,0:T(2,128)S(1)} %copy-done.17, f32[2,1024,2048]{2,1,0:T(8,128)} %get-tuple-element.43, f32[2,2048]{1,0:T(2,128)S(1)} %copy-done.14, bf16[2,1024,2048]{2,1,0:T(8,128)(2,1)} %fusion.1, bf16[2048,2048]{1,0:T(8,128)(2,1)} %param.13, ...), kind=kOutput, calls=%fused_computation.86 | convolution fusion | flops 17217609728 | bytes 50413568 | tf_op jit(solution)/shard_map/vnd,kd->vnk/dot_general | solution.py:67
  683.1 32.2 %psum.75 = f32[2,2,2048]{2,1,0:T(2,128)S(1)} all-reduce(f32[2,2,2048]{2,1,0:T(2,128)S(1)} %pad_maximum_fusion.5), channel_id=1, replica_groups=mesh['data'=16] {'data'}, use_global_device_ids=true, to_apply=%region_16.17 | all-reduce | flops 8192 | bytes 65536 | tf_op jit(solution)/shard_map/psum | solution.py:26
  716.0 12.2 %multiply_convert_fusion.1 = bf16[2,1024,2048]{2,1,0:T(8,128)(2,1)S(1)} fusion(f32[2,1024,2048]{2,1,0:T(8,128)} %get-tuple-element.46, f32[2,1024,2048]{2,1,0:T(8,128)} %get-tuple-element.43, f32[2,2048]{1,0:T(2,128)S(1)} %get-tuple-element.32, f32[2,2048]{1,0:T(2,128)S(1)} %get-tuple-element.33, f32[2,2048]{1,0:T(2,128)S(1)} %copy-done.15, ...), kind=kLoop, calls=%fused_computation.9 | loop fusion | flops 29360128 | bytes 42024960 | tf_op jit(solution)/shard_map/convert_element_type | solution.py:28
  731.4 22.9 %convolution_bitcast_fusion.1 = f32[2048,2048]{1,0:T(8,128)} fusion(bf16[2,1024,2048]{2,1,0:T(8,128)(2,1)S(1)} %multiply_convert_fusion.1, f32[2,1024,2048]{2,1,0:T(8,128)} %get-tuple-element.42, f32[2048]{0:T(1024)S(1)} %copy-done.25, f32[2,2048]{1,0:T(2,128)S(1)} %copy-done.12, f32[2,2048]{1,0:T(2,128)S(1)} %copy-done.9, f32[2048]{0:T(1024)S(1)} %copy-done.21), kind=kOutput, calls=%fused_computation.24 | convolution fusion | flops 17205035008 | bytes 41992192 | tf_op jit(solution)/shard_map/vnk,vnd->kd/dot_general | solution.py:69
  754.3 28.9 %fusion.42 = (f32[2,2048]{1,0:T(2,128)S(1)}, f32[2,2048]{1,0:T(2,128)S(1)}, f32[2,1024,2048]{2,1,0:T(8,128)}) fusion(f32[2,2048]{1,0:T(2,128)S(1)} %copy-done.12, f32[2,1024,2048]{2,1,0:T(8,128)} %get-tuple-element.42, f32[2,2048]{1,0:T(2,128)S(1)} %copy-done.9, bf16[2,1024,2048]{2,1,0:T(8,128)(2,1)} %copy-done.2, bf16[2048,2048]{1,0:T(8,128)(2,1)} %param.12, ...), kind=kOutput, calls=%fused_computation.85 | convolution fusion | flops 17217609728 | bytes 50413568 | tf_op jit(solution)/shard_map/vnd,kd->vnk/dot_general | solution.py:70
  783.3 33.4 %all-reduce = (f32[]{:T(128)}, f32[2,2,2048]{2,1,0:T(2,128)S(1)}) all-reduce(f32[]{:T(128)} %get-tuple-element.31, f32[2,2,2048]{2,1,0:T(2,128)S(1)} %pad_maximum_fusion.6), channel_id=1, replica_groups=mesh['data'=16] {'data'}, use_global_device_ids=true, to_apply=%region_7.0 | all-reduce | flops 8193 | bytes 65544 | tf_op jit(solution)/shard_map/psum | solution.py:61
  817.3 17.4 %fusion.19 = f32[384,2048]{1,0:T(8,128)} fusion(f32[2,1024,2048]{2,1,0:T(8,128)} %get-tuple-element.47, f32[2,1024,2048]{2,1,0:T(8,128)} %get-tuple-element.42, f32[2,2048]{1,0:T(2,128)S(1)} %get-tuple-element.34, f32[2,2048]{1,0:T(2,128)S(1)} %get-tuple-element.35, f32[2,2048]{1,0:T(2,128)S(1)} %copy-done.10, f32[2,2048]{1,0:T(2,128)S(1)} %copy-done.12, ...), kind=kOutput, calls=%fused_computation.38 | convolution fusion | flops 3251372032 | bytes 38354944 | tf_op jit(solution)/shard_map/vnf,vnd->fd/dot_general | solution.py:72
  838.5 338.5 %all-reduce.7.cloned.1.call-done = (f32[384,2048]{1,0:T(8,128)}, f32[2048,2048]{1,0:T(8,128)}, f32[2048,2048]{1,0:T(8,128)}) async-done(((f32[384,2048]{1,0:T(8,128)}, f32[2048,2048]{1,0:T(8,128)}, f32[2048,2048]{1,0:T(8,128)}), (f32[384,2048]{1,0:T(8,128)}, f32[2048,2048]{1,0:T(8,128)}, f32[2048,2048]{1,0:T(8,128)})) %all-reduce.7.cloned.1.call-update) | async-done | bytes 36700176 | tf_op jit(solution)/shard_map/psum | solution.py:73
  1181.1 13.6 %copy.42 = f32[2048,2048]{1,0:T(8,128)} copy(f32[2048,2048]{1,0:T(8,128)} %get-tuple-element.50) | data formatting | bytes 33554432
  (83 shorter events, 28.1 us)
Async XLA Ops:
  7.2 46.3 %copy-start.20 = (f32[2048]{0:T(1024)S(1)}, f32[2048]{0:T(1024)}, u32[]{:S(2)}) copy-start(f32[2048]{0:T(1024)} %param.14) | copy-start | bytes 24580
  7.2 47.0 %copy-start.24 = (f32[2048]{0:T(1024)S(1)}, f32[2048]{0:T(1024)}, u32[]{:S(2)}) copy-start(f32[2048]{0:T(1024)} %param.15) | copy-start | bytes 24580
  7.2 473.0 %all-reduce.5.cloned.1.call-start = ((), (), s32[]{:S(2)}) async-start(), calls=%async_computation | async-start | bytes 67108864 | tf_op jit(solution)/shard_map/psum | solution.py:61
  53.5 25.5 %copy-start.8 = (f32[2,2048]{1,0:T(2,128)}, f32[2,2048]{1,0:T(2,128)S(1)}, u32[]{:S(2)}) copy-start(f32[2,2048]{1,0:T(2,128)S(1)} %fusion.34) | copy-start | bytes 49156
  54.2 24.9 %copy-start.11 = (f32[2,2048]{1,0:T(2,128)}, f32[2,2048]{1,0:T(2,128)S(1)}, u32[]{:S(2)}) copy-start(f32[2,2048]{1,0:T(2,128)S(1)} %get-tuple-element.37) | copy-start | bytes 49156
  54.2 58.0 %copy-start.18 = (f32[2048]{0:T(1024)S(1)}, f32[2048]{0:T(1024)}, u32[]{:S(2)}) copy-start(f32[2048]{0:T(1024)} %param.16) | copy-start | bytes 24580
  54.2 58.7 %copy-start.22 = (f32[2048]{0:T(1024)S(1)}, f32[2048]{0:T(1024)}, u32[]{:S(2)}) copy-start(f32[2048]{0:T(1024)} %param.17) | copy-start | bytes 24580
  112.2 23.4 %copy-start.13 = (f32[2,2048]{1,0:T(2,128)}, f32[2,2048]{1,0:T(2,128)S(1)}, u32[]{:S(2)}) copy-start(f32[2,2048]{1,0:T(2,128)S(1)} %fusion.28) | copy-start | bytes 49156
  112.8 22.8 %copy-start.16 = (f32[2,2048]{1,0:T(2,128)}, f32[2,2048]{1,0:T(2,128)S(1)}, u32[]{:S(2)}) copy-start(f32[2,2048]{1,0:T(2,128)S(1)} %get-tuple-element.39) | copy-start | bytes 49156
  161.1 1015.9 %all-reduce.7.cloned.1.call-start = ((), (), s32[]{:S(2)}) async-start(), calls=%async_computation.1 | async-start | bytes 73400320 | tf_op jit(solution)/shard_map/psum | solution.py:73
  582.8 17.0 %copy-start.6 = (f32[2048,2]{0,1:T(2,128)}, f32[2048,2]{0,1:T(2,128)S(1)}, u32[]{:S(2)}) copy-start(f32[2048,2]{0,1:T(2,128)S(1)} %gather_fusion) | copy-start | bytes 49156
  599.8 29.2 %copy-start.14 = (f32[2,2048]{1,0:T(2,128)S(1)}, f32[2,2048]{1,0:T(2,128)}, u32[]{:S(2)}) copy-start(f32[2,2048]{1,0:T(2,128)} %copy-done.13) | copy-start | bytes 49156
  599.8 29.2 %copy-start.17 = (f32[2,2048]{1,0:T(2,128)S(1)}, f32[2,2048]{1,0:T(2,128)}, u32[]{:S(2)}) copy-start(f32[2,2048]{1,0:T(2,128)} %copy-done.16) | copy-start | bytes 49156
  599.9 29.2 %copy-start.19 = (f32[2048]{0:T(1024)S(1)}, f32[2048]{0:T(1024)}, u32[]{:S(2)}) copy-start(f32[2048]{0:T(1024)} %param.16) | copy-start | bytes 24580
  599.9 29.2 %copy-start.23 = (f32[2048]{0:T(1024)S(1)}, f32[2048]{0:T(1024)}, u32[]{:S(2)}) copy-start(f32[2048]{0:T(1024)} %param.17) | copy-start | bytes 24580
  654.3 61.6 %copy-start.15 = (f32[2,2048]{1,0:T(2,128)S(1)}, f32[2,2048]{1,0:T(2,128)}, u32[]{:S(2)}) copy-start(f32[2,2048]{1,0:T(2,128)} %get-tuple-element.38) | copy-start | bytes 49156
  716.0 15.4 %copy-start.9 = (f32[2,2048]{1,0:T(2,128)S(1)}, f32[2,2048]{1,0:T(2,128)}, u32[]{:S(2)}) copy-start(f32[2,2048]{1,0:T(2,128)} %copy-done.8) | copy-start | bytes 49156
  716.0 15.4 %copy-start.12 = (f32[2,2048]{1,0:T(2,128)S(1)}, f32[2,2048]{1,0:T(2,128)}, u32[]{:S(2)}) copy-start(f32[2,2048]{1,0:T(2,128)} %copy-done.11) | copy-start | bytes 49156
  716.0 15.4 %copy-start.21 = (f32[2048]{0:T(1024)S(1)}, f32[2048]{0:T(1024)}, u32[]{:S(2)}) copy-start(f32[2048]{0:T(1024)} %param.14) | copy-start | bytes 24580
  754.3 63.0 %copy-start.4 = (bf16[1024,384]{1,0:T(8,128)(2,1)S(1)}, bf16[1024,384]{1,0:T(8,128)(2,1)}, u32[]{:S(2)}) copy-start(bf16[1024,384]{1,0:T(8,128)(2,1)} %param.10) | copy-start | bytes 2359300
  754.3 63.0 %copy-start.5 = (bf16[1024,384]{1,0:T(8,128)(2,1)S(1)}, bf16[1024,384]{1,0:T(8,128)(2,1)}, u32[]{:S(2)}) copy-start(bf16[1024,384]{1,0:T(8,128)(2,1)} %param.9) | copy-start | bytes 2359300
  754.3 63.0 %copy-start.10 = (f32[2,2048]{1,0:T(2,128)S(1)}, f32[2,2048]{1,0:T(2,128)}, u32[]{:S(2)}) copy-start(f32[2,2048]{1,0:T(2,128)} %get-tuple-element.36) | copy-start | bytes 49156
  1177.0 17.6 %slice-start = ((s8[16777216]{0:T(1024)(128)(4,1)}), s8[4194304]{0:T(1024)(128)(4,1)S(1)}, s32[]{:S(2)}) async-start(s8[16777216]{0:T(1024)(128)(4,1)} %bitcast.101), calls=%async_computation.2 | async-start | bytes 8388608
  1181.1 21.5 %copy-start.1 = (bf16[384,2048]{1,0:T(8,128)(2,1)S(1)}, bf16[384,2048]{1,0:T(8,128)(2,1)}, u32[]{:S(2)}) copy-start(bf16[384,2048]{1,0:T(8,128)(2,1)} %param.11) | copy-start | bytes 4718596
  (8 other events, 66.5 us)
Sparse Core Ops, SparseCore 0:
  161.2 318.9 all-reduce.4
  834.8 342.1 all-reduce.6
where the time goes:
time: 1220 us; the launch traced here: 1210 us
  waiting for transfers between devices  609 us (50%)
  matrix products  249 us (20%)
  blocking collectives  168 us (14%)
  local copies, waits for them, and re-layouts  113 us (9%)
  other arithmetic  53.2 us (4%)
  between operations  18.4 us (2%)
    psum x1, waiting for transfers between devices, local_step(): lax.psum((grad_one, grad_two, grad_three), 'data')  338 us
    psum x1, waiting for transfers between devices, local_step(): lax.psum((jnp.sum(z_views, axis=1, dtype=jnp.float32), jnp.einsum('woe,wo...  271 us
    psum x2, blocking collectives, layer_forward(): lax.psum(jnp.stack([jnp.sum(pre_act, axis=1), jnp.sum(pre_act * pre_act,...  67.9 us
    psum x2, blocking collectives, local_step(): lax.psum((jnp.sum(z_views, axis=1, dtype=jnp.float32), jnp.einsum('woe,wo...  67.4 us
    div x1, local copies, waits for them, and re-layouts, loss_from_stats(): (gram_mat - all_rows * col_mu[:, :, None] * col_mu[:, None, :]) / (all_ro...  55 us
    dot_general x2, matrix products, layer_forward(): jnp.einsum('vnk,kd->vnd', x_in, weight, preferred_element_type=jnp.float32)  34.9 us
    unnamed x63, local copies, waits for them, and re-layouts  34.1 us
    psum x1, blocking collectives, layer_backward(): lax.psum(jnp.stack([jnp.sum(d_act, axis=1), jnp.sum(d_act * normed, axis=...  32.2 us
  transfers between devices with their start and end apart: 2, of which 2 were waited for; matrix products, arithmetic and copies ran while one was open for 1% of the time, Pallas kernels for 0%

commit v1 on v0

v1 whole, which is shorter than its diff:
```python
import jax
import jax.numpy as jnp
from jax import lax
from jax.experimental import pallas as pl
from jax.experimental.pallas import tpu as pltpu
from jax.sharding import PartitionSpec as P

BN_EPS = 1e-5
STD_EPS = 1e-4
INV_WEIGHT = 2.0
VAR_WEIGHT = 1.0
COV_WEIGHT = 2.0

N_DEV = 16
ROWS = 1024
DIM = 2048
ALL_ROWS = N_DEV * ROWS
MESH = pl.DeviceIdType.MESH
VMEM_LIMIT = 64 * 1024 * 1024 - 128 * 1024

ORDERS = ((0, 1, 2), (1, 2, 0), (2, 0, 1))
Q_ORDER = (7, 6, 5, 3, 4, 2, 1, 0)


def sent_stage(q, k):
    for s, d in enumerate(ORDERS[k]):
        if (q >> d) & 1:
            return s
    return 3


def last_stage(q, k):
    last = -1
    for s, d in enumerate(ORDERS[k]):
        if (q >> d) & 1:
            last = s
    return last


class Place:
    def __init__(self):
        self.me = lax.axis_index('data')
        self.core = self.me % 2
        self.bits = ((self.me // 2) % 2, (self.me // 4) % 2, self.me // 8)
        self.partner = self.me + 1 - 2 * self.core
        self.near = tuple(self.me + (2 << d) - (4 << d) * self.bits[d] for d in range(3))

    def chip(self, q):
        p = 0
        for d in range(3):
            b = self.bits[d]
            p = p + ((1 - b) if (q >> d) & 1 else b) * (1 << d)
        return p


def entry_barrier(me):
    sem = pltpu.get_barrier_semaphore()
    for k in range(1, N_DEV):
        pl.semaphore_signal(sem, inc=1, device_id=((me + k) % N_DEV,), device_id_type=MESH)
    pl.semaphore_wait(sem, N_DEV - 1)


def rcopy(src, dst, ssem, rsem, dev):
    return pltpu.make_async_remote_copy(src_ref=src, dst_ref=dst, send_sem=ssem, recv_sem=rsem,
                                        device_id=(dev,), device_id_type=MESH)


def lanes(i):
    return pl.ds(pl.multiple_of(i * 128, 128), 128)


class SmallSum:
    def __init__(self, me, x_ref, o_ref, slots, sems):
        self.me, self.x, self.o, self.slots, self.sems = me, x_ref, o_ref, slots, sems

    def out_copy(self, k):
        peer = (self.me + k) % N_DEV
        return rcopy(self.x.at[:, lanes(peer)], self.slots.at[self.me], self.sems.at[0, peer],
                     self.sems.at[1, self.me], peer)

    def in_copy(self, k):
        src = (self.me + k) % N_DEV
        return rcopy(self.x.at[:, lanes(src)], self.slots.at[src], self.sems.at[0, src], self.sems.at[1, src], src)

    def out_bcast(self, k):
        peer = (self.me + k) % N_DEV
        mine = self.o.at[:, lanes(self.me)]
        return rcopy(mine, mine, self.sems.at[2, peer], self.sems.at[3, self.me], peer)

    def in_bcast(self, k):
        src = (self.me + k) % N_DEV
        theirs = self.o.at[:, lanes(src)]
        return rcopy(theirs, theirs, self.sems.at[2, src], self.sems.at[3, src], src)

    def start(self):
        for k in range(1, N_DEV):
            self.out_copy(k).start()
        self.slots[self.me] = self.x[:, lanes(self.me)]

    def middle(self):
        for k in range(1, N_DEV):
            self.in_copy(k).wait_recv()
        total = self.slots[0]
        for s in range(1, N_DEV):
            total = total + self.slots[s]
        self.o[:, lanes(self.me)] = total
        for k in range(1, N_DEV):
            self.out_bcast(k).start()

    def finish(self):
        for k in range(1, N_DEV):
            self.in_bcast(k).wait_recv()
        for k in range(1, N_DEV):
            self.out_copy(k).wait_send()
            self.out_bcast(k).wait_send()


SMALL_SCRATCH = [pltpu.VMEM((N_DEV, 8, 128), jnp.float32), pltpu.SemaphoreType.DMA((4, N_DEV))]


def small_sum_kernel(x_ref, o_ref, slots, sems):
    me = lax.axis_index('data')
    entry_barrier(me)
    s = SmallSum(me, x_ref, o_ref, slots, sems)
    s.start()
    s.middle()
    s.finish()


def small_sum(x, cid):
    vm = pl.BlockSpec(memory_space=pltpu.VMEM)
    return pl.pallas_call(
        small_sum_kernel, out_shape=jax.ShapeDtypeStruct((8, DIM), jnp.float32),
        in_specs=[vm], out_specs=vm, scratch_shapes=SMALL_SCRATCH,
        compiler_params=pltpu.CompilerParams(collective_id=cid, has_side_effects=True),
        cost_estimate=pl.CostEstimate(flops=8_000_000, bytes_accessed=131072, transcendentals=0),
        name='small_sum')(x)


class Reduce:
    def __init__(self, place, own, land, ssem, rsem):
        self.place, self.own, self.land, self.ssem, self.rsem = place, own, land, ssem, rsem

    def copy(self, q, k):
        s = sent_stage(q, k)
        d = ORDERS[k][s]
        dst = q & ~(1 << d)
        return rcopy(self.own(q, k), self.land(s, dst, k), self.ssem.at[k, q], self.rsem.at[k, 8 * s + dst],
                     self.place.near[d])

    def arrive(self, q, k, s):
        self.copy(q | (1 << ORDERS[k][s]), k).wait_recv()
        own = self.own(q, k)
        own[...] = own[...] + self.land(s, q, k)[...]

    def stage(self, stage):
        for q in Q_ORDER:
            for k in range(3):
                if sent_stage(q, k) == stage:
                    for s in range(stage):
                        self.arrive(q, k, s)
                    if stage < 3:
                        self.copy(q, k).start()

    def drain(self):
        for k in range(3):
            for q in range(1, 8):
                self.copy(q, k).wait_send()


class Spread:
    def __init__(self, place, piece, ssem, rsem, csend, crecv, mine=None, lsem=None):
        self.place, self.piece, self.mine, self.lsem = place, piece, mine, lsem
        self.ssem, self.rsem, self.csend, self.crecv = ssem, rsem, csend, crecv

    def source(self, q, k):
        if q == 0 and self.mine is not None:
            return self.mine(k)
        return self.piece(self.place.chip(q), self.place.core, k)

    def copy(self, q, k, u):
        d = ORDERS[k][u]
        ref = self.piece(self.place.chip(q), self.place.core, k)
        return rcopy(self.source(q, k), ref, self.ssem.at[k, 3 * q + u], self.rsem.at[k, q | (1 << d)],
                     self.place.near[d])

    def to_partner(self, q, k):
        ref = self.piece(self.place.chip(q), self.place.core, k)
        return rcopy(self.source(q, k), ref, self.csend.at[k, q], self.crecv.at[k, q], self.place.partner)

    def keep(self, k):
        ref = self.piece(self.place.chip(0), self.place.core, k)
        return pltpu.make_async_copy(self.mine(k), ref, self.lsem.at[k])

    def from_partner(self, q, k):
        ref = self.piece(self.place.chip(q), 1 - self.place.core, k)
        return rcopy(ref, ref, self.csend.at[k, q], self.crecv.at[k, q], self.place.partner)

    def start(self, k):
        for u in range(3):
            self.copy(0, k, u).start()
        self.to_partner(0, k).start()
        if self.mine is not None:
            self.keep(k).start()

    def run(self, stages=(0, 1, 2)):
        for stage in stages:
            for q in range(1, 8):
                for k in range(3):
                    if last_stage(q, k) != stage:
                        continue
                    d = ORDERS[k][stage]
                    ref = self.piece(self.place.chip(q), self.place.core, k)
                    rcopy(ref, ref, self.ssem.at[k, 3 * q], self.rsem.at[k, q], self.place.near[d]).wait_recv()
                    for u in range(stage + 1, 3):
                        self.copy(q, k, u).start()
                    self.to_partner(q, k).start()

    def finish(self):
        for q in range(8):
            for k in range(3):
                self.from_partner(q, k).wait_recv()
        for k in range(3):
            if self.mine is not None:
                self.keep(k).wait()
        for q in range(8):
            for k in range(3):
                for u in range(last_stage(q, k) + 1, 3):
                    self.copy(q, k, u).wait_send()
                self.to_partner(q, k).wait_send()


def land_slot(s, q, k):
    order = [x for x in range(8) if sent_stage(x, k) > s]
    return (0, 4, 6)[s] + order.index(q)


def gram_kernel(z_ref, st_ref, pack_ref, tot_ref, loss_ref, gbuf, cbuf, rbuf, slots, sems, csem, rs_s, rs_r,
                ag_s, ag_r, agc_s, agc_r):
    place = Place()
    me, core = place.me, place.core
    entry_barrier(me)
    small = SmallSum(me, st_ref, tot_ref, slots, sems)
    small.start()

    def to_partner(q):
        return rcopy(gbuf.at[1, q, pl.ds(0, 9)], cbuf.at[q], csem.at[0, q], csem.at[1, q], place.partner)

    red = Reduce(place, lambda q, k: gbuf.at[0, q, pl.ds(3 * k, 3)],
                 lambda s, q, k: rbuf.at[k, land_slot(s, q, k)], rs_s, rs_r)

    def core_sum(q):
        to_partner(q).wait_recv()
        mine = gbuf.at[0, q, pl.ds(0, 9)]
        mine[...] = mine[...] + cbuf[q]
        for k in range(3):
            if sent_stage(q, k) == 0:
                red.copy(q, k).start()

    for i, q in enumerate(Q_ORDER):
        p = place.chip(q)

        @pl.loop(0, 2)
        def _(v):
            left = z_ref[v, :, pl.ds(pl.multiple_of(p * 256, 256), 256)]

            @pl.loop(0, 5)
            def _(b):
                right = z_ref[v, :, pl.ds(pl.multiple_of(((p + b) % 8) * 256, 256), 256)]
                out = lax.dot_general(left, right, (((0,), (0,)), ((), ())), preferred_element_type=jnp.float32)
                gbuf[core, q, 2 * b, v] = out[:128, :128]
                gbuf[core, q, 2 * b + 1, v] = out[:128, 128:]
                gbuf[1 - core, q, (2 * b + 9) % 10, v] = out[128:, :128]
                gbuf[1 - core, q, 2 * b, v] = out[128:, 128:]

        to_partner(q).start()
        if i == 1:
            small.middle()
        if i > 0:
            core_sum(Q_ORDER[i - 1])
    core_sum(0)
    for s in (1, 2, 3):
        red.stage(s)
    small.finish()

    ag = Spread(place, lambda p, c, k: pack_ref.at[2 * p + c, pl.ds(3 * k, 3)], ag_s, ag_r, agc_s, agc_r)
    eye = lax.broadcasted_iota(jnp.int32, (128, 128), 0) == lax.broadcasted_iota(jnp.int32, (128, 128), 1)
    acc = jnp.zeros((128, 128), jnp.float32)
    mu_rows = [jnp.transpose(jnp.broadcast_to(tot_ref[pl.ds(v, 1), lanes(me)] / ALL_ROWS, (128, 128))) for v in range(2)]
    for j in range(9):
        for v in range(2):
            mu_cols = tot_ref[pl.ds(v, 1), lanes((me + j) % N_DEV)] / ALL_ROWS
            cov = (gbuf[0, 0, j, v] - ALL_ROWS * mu_rows[v] * mu_cols) / (ALL_ROWS - 1)
            grad = (2.0 * COV_WEIGHT) * cov
            if j == 0:
                std = jnp.sqrt(jnp.where(eye, cov, 1.0) + STD_EPS)
                hinge = (std < 1.0).astype(jnp.float32)
                acc = acc + jnp.where(eye, VAR_WEIGHT * jnp.maximum(1.0 - std, 0.0), COV_WEIGHT * cov * cov)
                grad = jnp.where(eye, -VAR_WEIGHT * hinge / (2.0 * std), grad)
            else:
                acc = acc + (COV_WEIGHT * (2.0 if j < 8 else 1.0)) * cov * cov
            pack_ref[me, j, v] = grad.astype(jnp.bfloat16)
        if j % 3 == 2:
            ag.start(j // 3)
    part = acc[0:8]
    for r in range(1, 16):
        part = part + acc[8 * r:8 * r + 8]
    loss_ref[...] = part
    ag.run()
    ag.finish()
    for q in range(8):
        to_partner(q).wait_send()
    red.drain()


def gram_loss(z, stats, cid):
    vm = pl.BlockSpec(memory_space=pltpu.VMEM)
    dma = pltpu.SemaphoreType.DMA
    return pl.pallas_call(
        gram_kernel,
        out_shape=(jax.ShapeDtypeStruct((N_DEV, 9, 2, 128, 128), jnp.bfloat16),
                   jax.ShapeDtypeStruct((8, DIM), jnp.float32),
                   jax.ShapeDtypeStruct((8, 128), jnp.float32)),
        in_specs=[vm, vm], out_specs=(vm, vm, vm),
        scratch_shapes=[pltpu.VMEM((2, 8, 10, 2, 128, 128), jnp.float32),
                        pltpu.VMEM((8, 9, 2, 128, 128), jnp.float32),
                        pltpu.VMEM((3, 7, 3, 2, 128, 128), jnp.float32)] + SMALL_SCRATCH
                       + [dma((2, 8)), dma((3, 8)), dma((3, 24)), dma((3, 24)), dma((3, 8)), dma((3, 8)), dma((3, 8))],
        compiler_params=pltpu.CompilerParams(collective_id=cid, has_side_effects=True, vmem_limit_bytes=VMEM_LIMIT),
        cost_estimate=pl.CostEstimate(flops=60_000_000_000, bytes_accessed=20_000_000, transcendentals=0),
        name='gram_loss')(z, stats)


def dz_kernel(z_ref, pack_ref, tot_ref, o_ref, gcol):
    v, t = pl.program_id(0), pl.program_id(1)
    for h in range(2):
        c = 2 * t + h
        col = pl.ds(128 * h, 128)
        for d in range(16):
            r = (c + 16 - d) % 16
            rows = pl.ds(pl.multiple_of(r * 128, 128), 128)
            if d <= 8:
                gcol[rows, col] = pack_ref[r, d, v]
            else:
                gcol[rows, col] = jnp.transpose(pack_ref[c, 16 - d, v])
    mu = jnp.broadcast_to(tot_ref[pl.ds(v, 1), :] / ALL_ROWS, (16, DIM))
    high = mu.astype(jnp.bfloat16).astype(jnp.float32)
    mid = (mu - high).astype(jnp.bfloat16).astype(jnp.float32)
    low = mu - high - mid
    row = lax.broadcasted_iota(jnp.int32, (16, DIM), 0)
    terms = jnp.where(row == 0, high, jnp.where(row == 1, mid, jnp.where(row == 2, low, 0.0))).astype(jnp.bfloat16)
    mean = jnp.sum(jnp.dot(terms, gcol[...], preferred_element_type=jnp.float32), axis=0, keepdims=True)
    sign = (1 - 2 * v).astype(jnp.float32) * (2.0 * INV_WEIGHT / ALL_ROWS)
    cols = pl.ds(pl.multiple_of(t * 256, 256), 256)

    @pl.loop(0, 4)
    def _(m):
        rows = pl.ds(pl.multiple_of(m * 256, 256), 256)
        acc = jnp.dot(z_ref[v, rows, :], gcol[...], preferred_element_type=jnp.float32)
        diff = z_ref[0, rows, cols].astype(jnp.float32) - z_ref[1, rows, cols].astype(jnp.float32)
        o_ref[0, rows, :] = ((2.0 / (ALL_ROWS - 1)) * (acc - mean) + sign * diff).astype(jnp.bfloat16)


def dz_call(z, pack, tot):
    full = lambda shape: pl.BlockSpec(shape, lambda v, t: (0,) * len(shape), pipeline_mode=pl.Buffered(1))
    return pl.pallas_call(
        dz_kernel, grid=(2, 8), out_shape=jax.ShapeDtypeStruct((2, ROWS, DIM), jnp.bfloat16),
        in_specs=[full((2, ROWS, DIM)), full((N_DEV, 9, 2, 128, 128)), full((8, DIM))],
        out_specs=pl.BlockSpec((1, ROWS, 256), lambda v, t: (v, 0, t)),
        scratch_shapes=[pltpu.VMEM((DIM, 256), jnp.bfloat16)],
        compiler_params=pltpu.CompilerParams(vmem_limit_bytes=40 * 1024 * 1024,
                                             dimension_semantics=('arbitrary', 'arbitrary')),
        cost_estimate=pl.CostEstimate(flops=2 * 2 * ROWS * DIM * DIM, bytes_accessed=27_000_000, transcendentals=0),
        name='dz')(z, pack, tot)


COLS = ((0, 640), (640, 640), (1280, 768))


def wgrad_kernel(x_ref, d_ref, w_ref, o_ref, p_ref, xt, part, cbuf, rbuf, csem, rs_s, rs_r, ag_s, ag_r, agc_s, agc_r, agl,
                 sum1, cbuf1, rbuf1, csem1, rs_s1, rs_r1, ag_s1, ag_r1, agc_s1, agc_r1, agl1):
    place = Place()
    me, core = place.me, place.core
    entry_barrier(me)

    def to_partner1(q):
        return rcopy(w_ref.at[:, lanes(2 * place.chip(q) + 1 - core)], cbuf1.at[q], csem1.at[0, q], csem1.at[1, q],
                     place.partner)

    red1 = Reduce(place, lambda q, k: sum1.at[q, pl.ds(128 * k, 128)],
                  lambda s, q, k: rbuf1.at[k, land_slot(s, q, k)], rs_s1, rs_r1)
    ag1 = Spread(place, lambda p, c, k: p_ref.at[pl.ds(128 * k, 128), lanes(2 * p + c)], ag_s1, ag_r1, agc_s1, agc_r1,
                 lambda k: sum1.at[0, pl.ds(128 * k, 128)], agl1)
    for q in Q_ORDER:
        to_partner1(q).start()

    def begin1():
        for q in Q_ORDER:
            to_partner1(q).wait_recv()
            sum1[q] = w_ref[:, lanes(2 * place.chip(q) + core)] + cbuf1[q]
            for k in range(3):
                if sent_stage(q, k) == 0:
                    red1.copy(q, k).start()

    def end1():
        red1.stage(3)
        for k in range(3):
            ag1.start(k)

    also = {0: begin1, 3: lambda: red1.stage(1), 5: lambda: red1.stage(2), 7: end1}

    def to_partner(q):
        return rcopy(part.at[1, q], cbuf.at[q], csem.at[0, q], csem.at[1, q], place.partner)

    def cols(k):
        return pl.ds(*COLS[k])

    red = Reduce(place, lambda q, k: part.at[0, q, :, cols(k)],
                 lambda s, q, k: rbuf.at[k, land_slot(s, q, k), :, pl.ds(0, COLS[k][1])], rs_s, rs_r)
    ag = Spread(place, lambda p, c, k: o_ref.at[pl.ds(pl.multiple_of((2 * p + c) * 128, 128), 128), cols(k)],
                ag_s, ag_r, agc_s, agc_r, lambda k: part.at[0, 0, :, cols(k)], agl)

    def core_sum(q):
        to_partner(q).wait_recv()

        @pl.loop(0, 8)
        def _(n):
            at = pl.ds(pl.multiple_of(n * 256, 256), 256)
            part[0, q, :, at] = part[0, q, :, at] + cbuf[q, :, at]

        for k in range(3):
            if sent_stage(q, k) == 0:
                red.copy(q, k).start()

    for i, q in enumerate(Q_ORDER):
        p = place.chip(q)

        @pl.loop(0, 8)
        def _(n):
            at = pl.ds(pl.multiple_of(n * 256, 256), 256)
            xt[:, at] = jnp.transpose(x_ref[at, pl.ds(pl.multiple_of(p * 256, 256), 256)])

        @pl.loop(0, 8)
        def _(n):
            at = pl.ds(pl.multiple_of(n * 256, 256), 256)
            out = jnp.dot(xt[...], d_ref[:, at], preferred_element_type=jnp.float32)
            part[core, q, :, at] = out[:128]
            part[1 - core, q, :, at] = out[128:]

        to_partner(q).start()
        if i in also:
            also[i]()
        if i > 0:
            core_sum(Q_ORDER[i - 1])
    core_sum(0)
    ag1.run((0,))
    red.stage(1)
    ag1.run((1,))
    red.stage(2)
    ag1.run((2,))
    red.stage(3)
    for k in range(3):
        ag.start(k)
    ag.run()
    ag1.finish()
    ag.finish()
    for q in range(8):
        to_partner(q).wait_send()
        to_partner1(q).wait_send()
    red.drain()
    red1.drain()


def wgrad(x, d, w, cid):
    vm = pl.BlockSpec(memory_space=pltpu.VMEM)
    hbm = pl.BlockSpec(memory_space=pl.ANY)
    dma = pltpu.SemaphoreType.DMA
    sems = [dma((2, 8)), dma((3, 8)), dma((3, 24)), dma((3, 24)), dma((3, 8)), dma((3, 8)), dma((3, 8)), dma((3,))]
    f32 = jnp.float32
    return pl.pallas_call(
        wgrad_kernel,
        out_shape=(jax.ShapeDtypeStruct((DIM, DIM), f32), jax.ShapeDtypeStruct((384, DIM), f32)),
        in_specs=[vm, vm, vm], out_specs=(hbm, hbm),
        scratch_shapes=[pltpu.VMEM((256, 2 * ROWS), jnp.bfloat16), pltpu.VMEM((2, 8, 128, DIM), f32),
                        pltpu.VMEM((8, 128, DIM), f32), pltpu.VMEM((3, 7, 128, 768), f32)] + sems
                       + [pltpu.VMEM((8, 384, 128), f32), pltpu.VMEM((8, 384, 128), f32),
                          pltpu.VMEM((3, 7, 128, 128), f32)] + sems,
        compiler_params=pltpu.CompilerParams(collective_id=cid, has_side_effects=True, vmem_limit_bytes=VMEM_LIMIT),
        cost_estimate=pl.CostEstimate(flops=100_000_000_000, bytes_accessed=60_000_000, transcendentals=0),
        name='wgrad')(x, d, w)


def pad_rows(*rows):
    x = jnp.concatenate(rows, axis=0)
    return jnp.pad(x, ((0, 8 - x.shape[0]), (0, 0)))


def layer_forward(x_in, weight, gain_vec, bias_vec, cid):
    pre_act = jnp.einsum('vnk,kd->vnd', x_in, weight, preferred_element_type=jnp.float32)
    moments = small_sum(pad_rows(jnp.sum(pre_act, axis=1), jnp.sum(pre_act * pre_act, axis=1)), cid)
    col_mean = moments[0:2] / ALL_ROWS
    col_var = moments[2:4] / ALL_ROWS - col_mean * col_mean
    inv_std = lax.rsqrt(col_var + BN_EPS)[:, None, :]
    normed = (pre_act - col_mean[:, None, :]) * inv_std
    act_val = gain_vec * normed + bias_vec
    return jnp.maximum(act_val, 0.0).astype(jnp.bfloat16), normed, act_val, inv_std


def layer_backward(d_out, normed, act_val, inv_std, gain_vec, cid, extra=None):
    d_act = jnp.where(act_val > 0.0, d_out, 0.0)
    rows = [jnp.sum(d_act, axis=1), jnp.sum(d_act * normed, axis=1)]
    if extra is not None:
        rows.append(extra)
    stat_sums = small_sum(pad_rows(*rows), cid)
    mean_d = (stat_sums[0:2] / ALL_ROWS)[:, None, :]
    mean_dn = (stat_sums[2:4] / ALL_ROWS)[:, None, :]
    d_pre = inv_std * gain_vec * (d_act - mean_d - normed * mean_dn)
    return d_pre.astype(jnp.bfloat16), stat_sums[2] + stat_sums[3], stat_sums[0] + stat_sums[1], stat_sums


def solution(mesh):
    def local_step(h_a, h_b, w_one, w_two, w_three, gain_one, bias_one, gain_two, bias_two):
        view_feats = jnp.stack([h_a, h_b])
        hidden_one, normed_one, act_one, inv_one = layer_forward(view_feats, w_one, gain_one, bias_one, 0)
        hidden_two, normed_two, act_two, inv_two = layer_forward(hidden_one, w_two, gain_two, bias_two, 1)
        z_views = jnp.einsum('vnk,kd->vnd', hidden_two, w_three, preferred_element_type=jnp.float32).astype(jnp.bfloat16)
        z_diff = z_views[0].astype(jnp.float32) - z_views[1].astype(jnp.float32)
        stats = pad_rows(jnp.sum(z_views, axis=1, dtype=jnp.float32), jnp.sum(z_diff * z_diff, axis=0)[None])
        pack, tot, loss_part = gram_loss(z_views, stats, 2)
        d_z = dz_call(z_views, pack, tot)
        grad_three = jnp.einsum('vnk,vnd->kd', hidden_two, d_z, preferred_element_type=jnp.float32)
        grad_three = lax.psum(grad_three, 'data')
        d_hidden_two = jnp.einsum('vnd,kd->vnk', d_z, w_three, preferred_element_type=jnp.float32)
        loss_row = jnp.pad(jnp.sum(loss_part, axis=0)[None], ((0, 0), (0, DIM - 128)))
        d_pre_two, gain_grad_two, bias_grad_two, sums = layer_backward(
            d_hidden_two, normed_two, act_two, inv_two, gain_two, 3, loss_row)
        loss_val = INV_WEIGHT * jnp.sum(tot[2]) / ALL_ROWS + jnp.sum(sums[4])
        d_hidden_one = jnp.einsum('vnd,kd->vnk', d_pre_two, w_two, preferred_element_type=jnp.float32)
        d_pre_one, gain_grad_one, bias_grad_one, _ = layer_backward(
            d_hidden_one, normed_one, act_one, inv_one, gain_one, 4)
        grad_one = jnp.einsum('vnf,vnd->fd', view_feats, d_pre_one, preferred_element_type=jnp.float32)
        flat = (2 * ROWS, DIM)
        grad_two, grad_one = wgrad(hidden_one.reshape(flat), d_pre_two.reshape(flat), grad_one, 5)
        return loss_val, grad_one, grad_two, grad_three, gain_grad_one, bias_grad_one, gain_grad_two, bias_grad_two

    row_spec = P('data', None)
    return jax.shard_map(local_step, mesh=mesh,
                         in_specs=(row_spec, row_spec, P(), P(), P(), P(), P(), P(), P()),
                         out_specs=(P(), P(), P(), P(), P(), P(), P(), P()),
                         check_vma=False)
```

time: 1220 us -> 657 us (0.54)
  waiting for transfers between devices: 609 us -> 0.02 us
  Pallas kernels: 0 us -> 406 us
  blocking collectives: 168 us -> 0 us
  matrix products: 249 us -> 158 us
  local copies, waits for them, and re-layouts: 113 us -> 34.2 us
  other arithmetic: 53.2 us -> 37.1 us
    psum x2 -> x1, waiting for transfers between devices: 609 us -> 0.01 us  [local_step(): grad_three = lax.psum(grad_three, 'data')]
    pallas_call x0 -> x7, Pallas kernels: none -> 406 us  [the longest x1 198 us: wgrad(): pl.pallas_call(wgrad_kernel, out_shape=(jax.ShapeDtypeStruct((DIM, DIM),...]
    psum x5 -> x0, blocking collectives: 168 us -> none  [the longest x2 67.9 us: layer_forward(): lax.psum(jnp.stack([jnp.sum(pre_act, axis=1), jnp.sum(pre_act * pre_act,...]
    dot_general x4 -> x0, matrix products: 91 us -> none  [the longest x1 29.1 us: loss_from_stats(): jnp.einsum('woe,wef->wof', z_views, g_hat, preferred_element_type=jnp.flo...]
    div x1 -> x0, local copies, waits for them, and re-layouts: 55 us -> none  [loss_from_stats(): (gram_mat - all_rows * col_mu[:, :, None] * col_mu[:, None, :]) / (all_ro...]
    gather x1 -> x0, local copies, waits for them, and re-layouts: 24.1 us -> none  [loss_from_stats(): diag_var = jnp.diagonal(cov_mat, axis1=1, axis2=2)]
    reduce_sum x4 -> x3, other arithmetic: 25.5 us -> 3.52 us  [the longest x1 2.04 us: local_step(): jnp.sum(z_diff * z_diff, axis=0)[None]]
    unnamed x63 -> x51, local copies, waits for them, and re-layouts: 34.1 us -> 33.5 us
  transfers between devices with their start and end apart: 2 -> 1, of which waited for: 2 -> 0; matrix products, arithmetic and copies ran while one was open for 1% -> 15% of each run, Pallas kernels for 0% -> 34%
where the time goes in v1:
time: 657 us; the launch traced here: 652 us
  Pallas kernels  406 us (62%)
  matrix products  158 us (24%)
  other arithmetic  37.1 us (6%)
  local copies, waits for them, and re-layouts  34.2 us (5%)
  between operations  17.2 us (3%)
    pallas_call x1, Pallas kernels, wgrad(): pl.pallas_call(wgrad_kernel, out_shape=(jax.ShapeDtypeStruct((DIM, DIM),...  198 us
    pallas_call x1, Pallas kernels, gram_loss(): pl.pallas_call(gram_kernel, out_shape=(jax.ShapeDtypeStruct((N_DEV, 9, 2,...  115 us
    pallas_call x4, Pallas kernels, small_sum(): pl.pallas_call(small_sum_kernel, out_shape=jax.ShapeDtypeStruct((8, DIM),...  48.6 us
    pallas_call x1, Pallas kernels, dz_call(): pl.pallas_call(dz_kernel, grid=(2, 8), out_shape=jax.ShapeDtypeStruct((2,...  43.5 us
    dot_general x2, matrix products, layer_forward(): jnp.einsum('vnk,kd->vnd', x_in, weight, preferred_element_type=jnp.float32)  36.8 us
    unnamed x51, local copies, waits for them, and re-layouts  33.5 us
    dot_general x1, matrix products, local_step(): jnp.einsum('vnd,kd->vnk', d_pre_two, w_two, preferred_element_type=jnp.fl...  29.2 us
    dot_general x1, matrix products, local_step(): jnp.einsum('vnd,kd->vnk', d_z, w_three, preferred_element_type=jnp.float32)  28.7 us
  transfers between devices with their start and end apart: 1, of which 0 were waited for; matrix products, arithmetic and copies ran while one was open for 15% of the time, Pallas kernels for 34%

profile of v1, /device:TPU:0, one launch (start us, length us, event | category | flops | bytes accessed | tf_op | source)
XLA Modules:
  0.0 652.1 jit_solution(889808024881613502)
XLA Ops:
  7.2 12.8 %fusion.26 = (f32[2,2048]{1,0:T(2,128)S(1)}, f32[2,2048]{1,0:T(2,128)S(1)}, f32[2,1024,2048]{2,1,0:T(8,128)}) fusion(bf16[384,2048]{1,0:T(8,128)(2,1)} %param.11, bf16[1,1024,384]{2,1,0:T(8,128)(2,1)} %bitcast.51, bf16[1,1024,384]{2,1,0:T(8,128)(2,1)} %bitcast.53), kind=kOutput, calls=%fused_computation.62 | convolution fusion | flops 3234586624 | bytes 19955712 | tf_op jit(solution)/shard_map/vnk,kd->vnd/dot_general | solution.py:499
  20.7 14.6 %small_sum.4 = f32[8,2048]{1,0:T(8,128)} custom-call(f32[8,2048]{1,0:T(8,128)} %select_maximum_fusion.4.x_ref), custom_call_target="tpu_custom_call" | custom-call | flops 8000000 | bytes 131072 | tf_op jit(solution)/shard_map/small_sum/pallas_call | solution.py:132
  37.4 8.0 %maximum_convert_fusion.1 = bf16[2,1024,2048]{2,1,0:T(8,128)(2,1)S(1)} fusion(f32[2,1024,2048]{2,1,0:T(8,128)} %get-tuple-element.41, f32[2048]{0:T(1024)S(1)} %copy-done.15, f32[2,2048]{1,0:T(2,128)S(1)} %get-tuple-element.32, f32[2,2048]{1,0:T(2,128)S(1)} %get-tuple-element.33, f32[2048]{0:T(1024)S(1)} %copy-done.13), kind=kLoop, calls=%fused_computation.9 | loop fusion | flops 25165824 | bytes 25214976 | tf_op jit(solution)/shard_map/convert_element_type | solution.py:506
  45.4 24.1 %fusion.25 = (f32[2,2048]{1,0:T(2,128)S(1)}, f32[2,2048]{1,0:T(2,128)S(1)}, f32[2,1024,2048]{2,1,0:T(8,128)}) fusion(bf16[2,1024,2048]{2,1,0:T(8,128)(2,1)S(1)} %maximum_convert_fusion.1, bf16[2048,2048]{1,0:T(8,128)(2,1)} %param.12), kind=kOutput, calls=%fused_computation.61 | convolution fusion | flops 17192443904 | bytes 33587200 | tf_op jit(solution)/shard_map/vnk,kd->vnd/dot_general | solution.py:499
  70.2 10.3 %small_sum.5 = f32[8,2048]{1,0:T(8,128)} custom-call(f32[8,2048]{1,0:T(8,128)} %select_maximum_fusion.3.x_ref), custom_call_target="tpu_custom_call" | custom-call | flops 8000000 | bytes 131072 | tf_op jit(solution)/shard_map/small_sum/pallas_call | solution.py:132
  82.0 22.8 %convert_reduce_fusion = (f32[2,2048]{1,0:T(2,128)S(1)}, bf16[2,1024,2048]{2,1,0:T(8,128)(2,1)S(1)}) fusion(bf16[2048,2048]{1,0:T(8,128)(2,1)} %param.13, f32[2,1024,2048]{2,1,0:T(8,128)} %get-tuple-element.42, f32[2048]{0:T(1024)S(1)} %copy-done.19, f32[2,2048]{1,0:T(2,128)S(1)} %get-tuple-element.37, f32[2,2048]{1,0:T(2,128)S(1)} %get-tuple-element.38, ...), kind=kOutput, calls=%fused_computation.4 | convolution fusion | flops 17217613824 | bytes 33619968 | tf_op jit(solution)/shard_map/vnk,kd->vnd/dot_general | solution.py:526
  104.8 3.3 copy-done.2
  108.1 2.0 multiply_reduce_fusion.4
  110.8 115.5 %gram_loss.1 = (bf16[16,9,2,128,128]{4,3,2,1,0:T(8,128)(2,1)}, f32[8,2048]{1,0:T(8,128)}, f32[8,128]{1,0:T(8,128)}) custom-call(bf16[2,1024,2048]{2,1,0:T(8,128)(2,1)} %copy-done.2, f32[8,2048]{1,0:T(8,128)} %select_maximum_fusion.2.st_ref), custom_call_target="tpu_custom_call" | custom-call | flops 60000002048 | bytes 20000000 | tf_op jit(solution)/shard_map/gram_loss/pallas_call | solution.py:319
  227.2 43.5 %dz.1 = bf16[2,1024,2048]{2,1,0:T(8,128)(2,1)S(1)} custom-call(bf16[2,1024,2048]{2,1,0:T(8,128)(2,1)} %copy-done.2, bf16[16,9,2,128,128]{4,3,2,1,0:T(8,128)(2,1)} %get-tuple-element.14.pack_ref, f32[8,2048]{1,0:T(8,128)S(1)} %copy-done), custom_call_target="tpu_custom_call" | custom-call | flops 17179869184 | bytes 27000000 | tf_op jit(solution)/shard_map/dz/pallas_call | solution.py:366
  270.7 3.2 copy-done.1
  273.9 22.9 %convolution_bitcast_fusion = f32[2048,2048]{1,0:T(8,128)} fusion(bf16[2,1024,2048]{2,1,0:T(8,128)(2,1)S(1)} %dz.1, f32[2,1024,2048]{2,1,0:T(8,128)} %get-tuple-element.42, f32[2048]{0:T(1024)S(1)} %copy-done.19, f32[2,2048]{1,0:T(2,128)S(1)} %get-tuple-element.37, f32[2,2048]{1,0:T(2,128)S(1)} %get-tuple-element.38, f32[2048]{0:T(1024)S(1)} %copy-done.17), kind=kOutput, calls=%fused_computation.15 | convolution fusion | flops 17205035008 | bytes 41992192 | tf_op jit(solution)/shard_map/vnk,vnd->kd/dot_general | solution.py:531
  296.8 28.7 %fusion.24 = (f32[2,2048]{1,0:T(2,128)S(1)}, f32[2,2048]{1,0:T(2,128)S(1)}, f32[2,1024,2048]{2,1,0:T(8,128)}) fusion(f32[2,2048]{1,0:T(2,128)S(1)} %get-tuple-element.37, f32[2,1024,2048]{2,1,0:T(8,128)} %get-tuple-element.42, f32[2,2048]{1,0:T(2,128)S(1)} %get-tuple-element.38, bf16[2,1024,2048]{2,1,0:T(8,128)(2,1)} %copy-done.1, ...), kind=kOutput, calls=%fused_computation.60 | convolution fusion | flops 17217609728 | bytes 50413568 | tf_op jit(solution)/shard_map/vnd,kd->vnk/dot_general | solution.py:533
  326.3 11.9 %small_sum.6 = f32[8,2048]{1,0:T(8,128)} custom-call(f32[8,2048]{1,0:T(8,128)} %pad.26.x_ref), custom_call_target="tpu_custom_call" | custom-call | flops 8000000 | bytes 131072 | tf_op jit(solution)/shard_map/small_sum/pallas_call | solution.py:132
  339.2 15.1 %multiply_convert_fusion.1 = bf16[2,1024,2048]{2,1,0:T(8,128)(2,1)} fusion(f32[2,1024,2048]{2,1,0:T(8,128)} %get-tuple-element.45, f32[2,1024,2048]{2,1,0:T(8,128)} %get-tuple-element.42, f32[2,2048]{1,0:T(2,128)S(1)} %get-tuple-element.40, f32[2,2048]{1,0:T(2,128)S(1)} %get-tuple-element.39, f32[2,2048]{1,0:T(2,128)S(1)} %copy-done.12, ...), kind=kLoop, calls=%fused_computation.2 | loop fusion | flops 29360128 | bytes 42024960 | tf_op jit(solution)/shard_map/convert_element_type | solution.py:518
  354.4 29.2 %fusion.23 = (f32[2,2048]{1,0:T(2,128)S(1)}, f32[2,2048]{1,0:T(2,128)S(1)}, f32[2,1024,2048]{2,1,0:T(8,128)}) fusion(f32[2,2048]{1,0:T(2,128)S(1)} %copy-done.8, f32[2,1024,2048]{2,1,0:T(8,128)} %get-tuple-element.41, f32[2,2048]{1,0:T(2,128)S(1)} %copy-done.10, bf16[2,1024,2048]{2,1,0:T(8,128)(2,1)} %multiply_convert_fusion.1, ...), kind=kOutput, calls=%fused_computation.59 | convolution fusion | flops 17217609728 | bytes 50413568 | tf_op jit(solution)/shard_map/vnd,kd->vnk/dot_general | solution.py:538
  384.2 11.8 %small_sum.7 = f32[8,2048]{1,0:T(8,128)} custom-call(f32[8,2048]{1,0:T(8,128)} %select_maximum_fusion.x_ref), custom_call_target="tpu_custom_call" | custom-call | flops 8000000 | bytes 131072 | tf_op jit(solution)/shard_map/small_sum/pallas_call | solution.py:132
  397.0 17.4 %fusion.16.w_ref = f32[384,2048]{1,0:T(8,128)} fusion(f32[2,1024,2048]{2,1,0:T(8,128)} %get-tuple-element.46, f32[2,1024,2048]{2,1,0:T(8,128)} %get-tuple-element.41, f32[2,2048]{1,0:T(2,128)S(1)} %get-tuple-element.35, f32[2,2048]{1,0:T(2,128)S(1)} %get-tuple-element.34, f32[2,2048]{1,0:T(2,128)S(1)} %copy-done.11, f32[2,2048]{1,0:T(2,128)S(1)} %copy-done.8, ...), kind=kOutput, calls=%fused_computation.27 | convolution fusion | flops 3251372032 | bytes 38354944 | tf_op jit(solution)/shard_map/vnf,vnd->fd/dot_general | solution.py:541
  414.4 198.2 %wgrad.1 = (f32[2048,2048]{1,0:T(8,128)}, f32[384,2048]{1,0:T(8,128)}) custom-call(bf16[2048,2048]{1,0:T(8,128)(2,1)} %bitcast.50, bf16[2048,2048]{1,0:T(8,128)(2,1)} %bitcast.49, f32[384,2048]{1,0:T(8,128)} %fusion.16.w_ref), custom_call_target="tpu_custom_call" | custom-call | flops 99999997952 | bytes 60000000 | tf_op jit(solution)/shard_map/wgrad/pallas_call | solution.py:480
  616.6 1.6 slice_add_fusion.2
  618.2 4.1 copy.24
  622.2 13.6 %copy.25 = f32[2048,2048]{1,0:T(8,128)} copy(f32[2048,2048]{1,0:T(8,128)} %get-tuple-element.57) | data formatting | bytes 33554432
  635.8 1.7 slice-done.3
  637.6 6.2 copy.26
  (62 shorter events, 12.5 us)
Async XLA Ops:
  7.2 28.1 %copy-start.13 = (f32[2048]{0:T(1024)S(1)}, f32[2048]{0:T(1024)}, u32[]{:S(2)}) copy-start(f32[2048]{0:T(1024)} %param.14) | copy-start | bytes 24580
  7.2 30.2 %copy-start.15 = (f32[2048]{0:T(1024)S(1)}, f32[2048]{0:T(1024)}, u32[]{:S(2)}) copy-start(f32[2048]{0:T(1024)} %param.15) | copy-start | bytes 24580
  7.2 611.0 %all-reduce.8.cloned.1.call-start = ((), (), s32[]{:S(2)}) async-start(), calls=%async_computation | async-start | bytes 33554432 | tf_op jit(solution)/shard_map/psum | solution.py:532
  36.8 0.6 copy-start.9
  45.4 24.1 %copy-start.3 = (bf16[2,1024,2048]{2,1,0:T(8,128)(2,1)}, bf16[2,1024,2048]{2,1,0:T(8,128)(2,1)S(1)}, u32[]{:S(2)}) copy-start(bf16[2,1024,2048]{2,1,0:T(8,128)(2,1)S(1)} %maximum_convert_fusion.1) | copy-start | bytes 25165828
  45.4 35.1 %copy-start.17 = (f32[2048]{0:T(1024)S(1)}, f32[2048]{0:T(1024)}, u32[]{:S(2)}) copy-start(f32[2048]{0:T(1024)} %param.16) | copy-start | bytes 24580
  45.4 36.6 %copy-start.19 = (f32[2048]{0:T(1024)S(1)}, f32[2048]{0:T(1024)}, u32[]{:S(2)}) copy-start(f32[2048]{0:T(1024)} %param.17) | copy-start | bytes 24580
  104.8 3.3 copy-start.2
  226.3 0.8 copy-start
  270.7 3.2 copy-start.1
  296.8 28.8 %copy-start.18 = (f32[8,128]{1,0:T(8,128)S(1)}, f32[8,128]{1,0:T(8,128)}, u32[]{:S(2)}) copy-start(f32[8,128]{1,0:T(8,128)} %get-tuple-element.15) | copy-start | bytes 12292
  296.8 42.3 %copy-start.12 = (f32[2,2048]{1,0:T(2,128)S(1)}, f32[2,2048]{1,0:T(2,128)}, u32[]{:S(2)}) copy-start(f32[2,2048]{1,0:T(2,128)} %get-tuple-element.36) | copy-start | bytes 49156
  339.1 15.2 %copy-start.8 = (f32[2,2048]{1,0:T(2,128)S(1)}, f32[2,2048]{1,0:T(2,128)}, u32[]{:S(2)}) copy-start(f32[2,2048]{1,0:T(2,128)} %copy-done.7) | copy-start | bytes 49156
  339.1 15.2 %copy-start.10 = (f32[2,2048]{1,0:T(2,128)S(1)}, f32[2,2048]{1,0:T(2,128)}, u32[]{:S(2)}) copy-start(f32[2,2048]{1,0:T(2,128)} %copy-done.9) | copy-start | bytes 49156
  339.2 15.2 %copy-start.14 = (f32[2048]{0:T(1024)S(1)}, f32[2048]{0:T(1024)}, u32[]{:S(2)}) copy-start(f32[2048]{0:T(1024)} %param.14) | copy-start | bytes 24580
  339.2 15.2 %copy-start.16 = (f32[2048]{0:T(1024)S(1)}, f32[2048]{0:T(1024)}, u32[]{:S(2)}) copy-start(f32[2048]{0:T(1024)} %param.15) | copy-start | bytes 24580
  354.3 42.6 %copy-start.4 = (bf16[1024,384]{1,0:T(8,128)(2,1)S(1)}, bf16[1024,384]{1,0:T(8,128)(2,1)}, u32[]{:S(2)}) copy-start(bf16[1024,384]{1,0:T(8,128)(2,1)} %param.10) | copy-start | bytes 2359300
  354.4 42.6 %copy-start.5 = (bf16[1024,384]{1,0:T(8,128)(2,1)S(1)}, bf16[1024,384]{1,0:T(8,128)(2,1)}, u32[]{:S(2)}) copy-start(bf16[1024,384]{1,0:T(8,128)(2,1)} %param.9) | copy-start | bytes 2359300
  354.4 42.6 %copy-start.11 = (f32[2,2048]{1,0:T(2,128)S(1)}, f32[2,2048]{1,0:T(2,128)}, u32[]{:S(2)}) copy-start(f32[2,2048]{1,0:T(2,128)} %get-tuple-element.31) | copy-start | bytes 49156
  414.4 200.3 %copy-start.6 = (f32[8,2048]{1,0:T(8,128)S(1)}, f32[8,2048]{1,0:T(8,128)}, u32[]{:S(2)}) copy-start(f32[8,2048]{1,0:T(8,128)} %small_sum.6) | copy-start | bytes 196612
  618.2 17.6 %slice-start = ((s8[16777216]{0:T(1024)(128)(4,1)}), s8[4194304]{0:T(1024)(128)(4,1)S(1)}, s32[]{:S(2)}) async-start(s8[16777216]{0:T(1024)(128)(4,1)} %bitcast.47), calls=%async_computation.1 | async-start | bytes 8388608
  622.2 13.6 %slice-start.1 = ((s8[16777216]{0:T(1024)(128)(4,1)}), s8[4194304]{0:T(1024)(128)(4,1)S(1)}, s32[]{:S(2)}) async-start(s8[16777216]{0:T(1024)(128)(4,1)} %bitcast.47), calls=%async_computation.2 | async-start | bytes 8388608
  622.2 13.6 %slice-start.2 = ((s8[16777216]{0:T(1024)(128)(4,1)}), s8[4194304]{0:T(1024)(128)(4,1)S(1)}, s32[]{:S(2)}) async-start(s8[16777216]{0:T(1024)(128)(4,1)} %bitcast.47), calls=%async_computation.3 | async-start | bytes 8388608
  622.2 15.3 %slice-start.3 = ((s8[16777216]{0:T(1024)(128)(4,1)}), s8[4194304]{0:T(1024)(128)(4,1)S(1)}, s32[]{:S(2)}) async-start(s8[16777216]{0:T(1024)(128)(4,1)} %bitcast.47), calls=%async_computation.4 | async-start | bytes 8388608
  (1 other events, 0.6 us)
Sparse Core Ops, SparseCore 0:
  296.9 224.6 all-reduce.7
